TPU v7x, 8 devices: a whole 2x2x1 slice. The times are simulated.
8 devices in a mesh: batch: 1 (over z), row: 2 (over y), col: 4 (over x, core).
Axes of the slice: x: 2, y: 2, z: 1, core: 2. Of those that a mesh axis runs over, the one named last changes fastest.
Arguments:
- left_op: bfloat16 [6144, 6144], P(('batch', 'row'), 'col')
- left_start: float32 [6144, 128], P(('batch', 'row', 'col'))
- right_op: bfloat16 [16384, 16384], P(('batch', 'row'), 'col')
- right_start: float32 [16384, 128], P(('batch', 'row', 'col'))
Outputs:
- output 1: float32 [6144, 128], P(('batch', 'row', 'col'))
- output 2: float32 [128, 128], P('batch')
- output 3: float32 [16384, 128], P(('batch', 'row', 'col'))
- output 4: float32 [128, 128], P('batch')
All inputs are finite; a program needn't handle non-finite values.
Results may differ from a plain program's by a relative error of at most 0.001.
Values are sent between devices in bfloat16 or wider.
A program may use at most 1 GiB of HBM per device.

v0:
```python
import jax
import jax.numpy as jnp
from jax import lax
from jax.experimental import pallas as pl
from jax.experimental.pallas import tpu as pltpu
from jax.sharding import PartitionSpec as P

SWEEPS = 4
S = 128
RING = 4
TILES = 4
CHUNKS = 2
STRAIGHT = 2
PANEL = 16
MESH = pl.DeviceIdType.MESH
F32, BF16 = jnp.float32, jnp.bfloat16
NT = (((1,), (1,)), ((), ()))
TN = (((0,), (0,)), ((), ()))


def dot(lhs, rhs):
    return jnp.dot(lhs, rhs, preferred_element_type=F32)


def dot_nt(lhs, rhs):
    return lax.dot_general(lhs, rhs, NT, preferred_element_type=F32)


def split(value):
    high = value.astype(BF16)
    rest = value - high.astype(F32)
    mid = rest.astype(BF16)
    low = (rest - mid.astype(F32)).astype(BF16)
    return high, mid, low


def remote(src, dst, send_sem, recv_sem, row, col):
    return pltpu.make_async_remote_copy(
        src_ref=src, dst_ref=dst, send_sem=send_sem, recv_sem=recv_sem,
        device_id={"row": row, "col": col}, device_id_type=MESH,
    )


def inverse_factor(ref):
    sub = lax.broadcasted_iota(jnp.int32, (PANEL, S), 0)
    lane = lax.broadcasted_iota(jnp.int32, (PANEL, S), 1)

    tall_row = lax.broadcasted_iota(jnp.int32, (S, S), 0)
    tall_lane = lax.broadcasted_iota(jnp.int32, (S, S), 1)

    def panel(p, carry):
        k0 = pl.multiple_of(p * PANEL, PANEL)
        inside = (tall_lane >= k0) & (tall_lane < k0 + PANEL) & (tall_row >= k0 + PANEL)
        at = lane - k0
        rows = ref[pl.ds(k0, PANEL), :]
        heads = jnp.stack(
            [
                jnp.broadcast_to(jnp.sum(jnp.where(at == j, rows, 0.0), axis=1, keepdims=True), (PANEL, S))
                for j in range(PANEL)
            ]
        )
        high, mid, low = split(jnp.where(at >= PANEL, rows, 0.0))
        cols = jnp.concatenate([high, mid, high, mid, high, low], axis=0)
        rows = jnp.where((at >= 0) & (at < PANEL), jnp.where(at == sub, 1.0, 0.0), rows)
        done = rows
        piv = heads[0, 0:1, :]
        for j in range(PANEL):
            here = sub == j
            root = lax.rsqrt(piv)
            inv = root * root
            done = jnp.where(here, rows * root, done)
            mult = jnp.where(here, 0.0, heads[0])
            if j < PANEL - 1:
                head_rows = heads[1:, j : j + 1, :] * inv
                piv = heads[1, j + 1 : j + 2, :] - heads[0, j + 1 : j + 2, :] * head_rows[0]
                heads = jnp.where(here[None], head_rows, heads[1:] - mult[None] * head_rows)
            scaled = rows[j : j + 1, :] * inv
            rows = jnp.where(here, scaled, rows - mult * scaled)
        high, mid, low = split(rows)
        rhs = jnp.concatenate([high, high, mid, mid, low, high], axis=0)
        change = lax.dot_general(cols, rhs, TN, preferred_element_type=F32)
        ref[...] = jnp.where(inside, 0.0, ref[...]) - change
        ref[pl.ds(k0, PANEL), :] = done
        return carry

    lax.fori_loop(0, S // PANEL, panel, 0)


class Op:
    def __init__(self, **refs):
        self.__dict__.update(refs)


def kernel(
    l_op, l_start, r_op, r_start,
    l_out, r_out, ray_out,
    l_a, r_a,
    l_xs, l_xt, l_mate_s, l_mate_r, l_side_s, l_side_r, l_hand, l_y, l_sp,
    r_xs, r_xt, r_ps, r_pr, r_y, r_sp, r_keep,
    g_loc, g_one, g_sum, g_two, g_m, g_fac,
    l_asem, r_asem,
    gs_sem, gr_sem, fs_sem, fr_sem, ps_sem, pr_sem, xs_sem, xr_sem, es_sem, er_sem,
    lgs_sem, lgr_sem, lhs_sem, lhr_sem, lms_sem, lmr_sem, lss_sem, lsr_sem,
    a1s_sem, a1r_sem, a2s_sem, a2r_sem, a3s_sem, a3r_sem,
):
    y = lax.axis_index("row")
    col = lax.axis_index("col")
    x = col // 2
    k = col % 2
    mate = x * 2 + (1 - k)
    l_n, r_n = l_op.shape[0] * 2, r_op.shape[0] * 2
    l_nb, r_nb = l_n // 8, r_n // 8
    tile = r_nb // TILES
    piece = r_nb // CHUNKS

    left = Op(i=0, n=l_n, nb=l_nb, y=l_y, sp=l_sp)
    right = Op(i=1, n=r_n, nb=r_nb, y=r_y, sp=r_sp)
    ops = [left, right]

    def r_fetch(t):
        half = jnp.where(t < TILES, 1 - y, y)
        start = pl.multiple_of(half * r_nb + (t % TILES) * tile, tile)
        return pltpu.make_async_copy(r_op.at[:, pl.ds(start, tile)], r_a.at[t % RING], r_asem.at[t % RING])

    for t in range(RING):
        r_fetch(t).start()
    l_load = pltpu.make_async_copy(l_op, l_a, l_asem)
    l_load.start()

    class Gather:
        def __init__(self, first):
            self.dest_row = y if first else x
            self.my_slot = 2 * x + k if first else 2 * k + y
            self.src = x if first else y
            self.slots = [2 * a + k if first else 2 * k + a for a in range(2)]
            self.other_slots = [2 * a + (1 - k) if first else 2 * (1 - k) + a for a in range(2)]
            self.sends_to_self = [(self.dest_row == y) & (x == a) for a in range(2)]
            self.gets_from_self = [(x == a) if first else ((x == y) & (y == a)) for a in range(2)]

        def copy(self, a, h, recv):
            return remote(
                r_xs.at[h], r_xt.at[self.my_slot, h], gs_sem.at[a, h], gr_sem.at[recv, h], self.dest_row, 2 * a + k
            )

        def forward(self, a, h, slots):
            ref = r_xt.at[slots[a], h]
            return remote(ref, ref, fs_sem.at[a, h], fr_sem.at[a, h], y, mate)

        def start(self, h):
            for a in range(2):

                @pl.when(self.sends_to_self[a])
                def _():
                    r_xt[self.my_slot, h] = r_xs[h]

                @pl.when(jnp.logical_not(self.sends_to_self[a]))
                def _():
                    self.copy(a, h, self.src).start()

        def finish(self):
            for h in range(CHUNKS):
                for a in range(2):

                    @pl.when(jnp.logical_not(self.gets_from_self[a]))
                    def _():
                        self.copy(0, h, a).wait_recv()

                    self.forward(a, h, self.slots).start()
                for a in range(2):
                    self.forward(a, h, self.other_slots).wait_recv()
                if h < CHUNKS - 1:
                    right_early(h)

        def drain(self):
            for h in range(CHUNKS):
                for a in range(2):
                    self.forward(a, h, self.slots).wait_send()

                    @pl.when(jnp.logical_not(self.sends_to_self[a]))
                    def _():
                        self.copy(a, h, self.src).wait_send()

    def left_copy(b, slot):
        return remote(l_xs, l_xt.at[slot], lgs_sem.at[b], lgr_sem.at[slot], b, 2 * y + x)

    def left_across(b):
        return remote(l_xs, l_hand, lgs_sem.at[b], lhr_sem, 1 - y, col)

    def left_hand_on():
        return remote(l_hand, l_xt.at[k], lhs_sem, lgr_sem.at[k], y, 2 * (1 - x) + x)

    def left_self(b):
        return (b == y) & (y == x) & (x == k)

    def left_start():
        for b in (1 - y, y):
            across = (b != y) & (x != y)

            @pl.when(left_self(b))
            def _():
                l_xt[k] = l_xs[...]

            @pl.when(across)
            def _():
                left_across(b).start()

            @pl.when(jnp.logical_not(left_self(b) | across))
            def _():
                left_copy(b, k).start()

    def left_relay():
        @pl.when(x == y)
        def _():
            left_across(0).wait_recv()
            left_hand_on().start()

    def left_finish():
        for slot in range(2):

            @pl.when(jnp.logical_not((y == x) & (x == k) & (k == slot)))
            def _():
                left_copy(0, slot).wait_recv()

    def left_drain():
        for b in range(2):

            @pl.when(jnp.logical_not(left_self(b)))
            def _():
                left_copy(b, k).wait_send()

        @pl.when(x == y)
        def _():
            left_hand_on().wait_send()

    def left_block(index):
        rows = pl.ds(pl.multiple_of(index * l_nb, l_nb), l_nb)
        return dot_nt(l_xt[0], l_a[rows, :l_nb]) + dot_nt(l_xt[1], l_a[rows, l_nb:])

    def left_mate(a):
        return remote(l_mate_s.at[a], l_mate_r.at[a], lms_sem.at[a], lmr_sem.at[a], y, mate)

    def left_side():
        return remote(l_side_s, l_side_r, lss_sem, lsr_sem, y, 2 * (1 - x) + k)

    def left_multiply():
        l_mate_s[1 - x] = left_block(2 * (1 - x) + (1 - k))
        left_mate(1 - x).start()
        l_side_s[...] = left_block(2 * (1 - x) + k)
        l_mate_s[x] = left_block(2 * x + (1 - k))
        left_mate(x).start()
        left_mate(1 - x).wait_recv()
        l_side_s[...] = l_side_s[...] + l_mate_r[1 - x]
        left_side().start()
        l_y[...] = left_block(2 * x + k)

    def left_reduce_finish():
        left_mate(x).wait_recv()
        l_y[...] = l_y[...] + l_mate_r[x]
        left_side().wait_recv()
        l_y[...] = l_y[...] + l_side_r[...]
        left_side().wait_send()
        for a in range(2):
            left_mate(a).wait_send()

    def right_send(t):
        return remote(r_ps.at[t], r_pr.at[t], ps_sem.at[t], pr_sem.at[t], 1 - y, col)

    def right_part(b, h):
        total = None
        for s in range(4):
            part = dot(r_xt[s, h], r_a[b, s * r_nb + h * piece : s * r_nb + (h + 1) * piece, :])
            total = part if total is None else total + part
        return total

    def right_early(h):
        def one(t, carry):
            if h == 0:
                r_fetch(t).wait()
                r_ps[t] = right_part(t, h)
            else:
                r_ps[t] = r_ps[t] + right_part(t, h)
            return carry

        lax.fori_loop(0, TILES, one, 0)

    def right_others(last):
        def one(t, carry):
            r_ps[t] = r_ps[t] + right_part(t, CHUNKS - 1)
            if not last:
                right_send(t).start()
            r_fetch(t + RING).start()
            return carry

        lax.fori_loop(0, TILES, one, 0)

    def right_own(last, begin, end):
        def one(i, carry):
            t = i + TILES
            r_fetch(t).wait()
            b = t % RING
            total = None
            for h in range(CHUNKS):
                part = right_part(b, h)
                total = part if total is None else total + part
            r_y[:, pl.ds(pl.multiple_of(i * tile, tile), tile)] = total
            if not last:
                r_fetch(lax.rem(t + RING, 2 * TILES)).start()
            return carry

        lax.fori_loop(begin, end, one, 0)

    def left_gram():
        with jax.named_scope("l_red"):
            left_reduce_finish()
        half = l_y[...].astype(BF16)
        pack(0, dot_nt(half, half))

    def right_reduce_finish():
        gram = None
        for t in range(TILES):
            if t == TILES - 1:
                left_gram()
            right_send(t).wait_recv()
            res = r_y[:, t * tile : (t + 1) * tile] + r_pr[t]
            r_y[:, t * tile : (t + 1) * tile] = res
            half = res.astype(BF16)
            part = dot_nt(half, half)
            gram = part if gram is None else gram + part
        pack(1, gram)
        for t in range(TILES):
            right_send(t).wait_send()

    low_lane = lax.broadcasted_iota(jnp.int32, (32, S), 1)
    tall_row = lax.broadcasted_iota(jnp.int32, (S, S), 0)
    tall_lane = lax.broadcasted_iota(jnp.int32, (S, S), 1)
    count = jnp.where(k == 0, float(l_n), float(r_n))

    def pack(i, gram):
        g_loc[i, :64, :] = gram[:64]
        g_loc[i, 64:96, :] = jnp.where(low_lane < 64, pltpu.roll(gram[64:96], 64, axis=1), gram[96:])

    def sum_across(par, rows, after_sends=lambda: None):
        part = pl.ds(0, rows)
        one = remote(g_loc.at[1 - k, part], g_one.at[par, part], a1s_sem.at[par], a1r_sem.at[par], y, mate)
        one.start()
        with jax.named_scope("ar_one"):
            one.wait_recv()
        g_sum[part, :] = g_loc[k, part, :] + g_one[par, part, :]
        twos = []
        for q in (2, 1, 0):
            yd = y + ((q + 1) // 2) * (1 - 2 * y)
            xd = x + ((q + 1) % 2) * (1 - 2 * x)
            two = remote(
                g_sum.at[part], g_two.at[par, q, part], a2s_sem.at[par, q], a2r_sem.at[par, q], yd, 2 * xd + k
            )
            two.start()
            twos.append(two)
        after_sends()
        with jax.named_scope("ar_two"):
            for two in twos:
                two.wait_recv()
        total = (g_sum[part, :] + g_two[par, 0, part, :]) + (g_two[par, 1, part, :] + g_two[par, 2, part, :])
        one.wait_send()
        for two in twos:
            two.wait_send()
        return total / count

    def hand_over(par, left_work, right_work):
        mine, other = g_fac.at[k], g_fac.at[1 - k]
        copy = remote(mine, mine, a3s_sem.at[par], a3r_sem.at[par], y, mate)
        back = remote(other, other, a3s_sem.at[par], a3r_sem.at[par], y, mate)
        copy.start()

        @pl.when(k == 0)
        def _():
            left_work()
            back.wait_recv()
            right_work()

        @pl.when(k == 1)
        def _():
            right_work()
            back.wait_recv()
            left_work()

        copy.wait_send()

    def factor(par):
        gram = sum_across(par, 96)
        g_m[:64, :] = gram[:64]
        g_m[64:96, :] = pltpu.roll(gram[64:], 64, axis=1)
        g_m[96:, :] = gram[64:]
        with jax.named_scope("chol"):
            inverse_factor(g_m)
        g_fac[k] = jnp.where(tall_lane <= tall_row, g_m[...], 0.0)

    def apply_piece(o, lhs, start, width):
        high, mid, low = split(o.y[:, start : start + width])
        rhs = jnp.concatenate([high, high, mid, mid, low, high], axis=0)
        return dot(lhs, rhs)

    def apply_lhs(o):
        high, mid, low = split(g_fac[o.i])
        return jnp.concatenate([high, mid, high, mid, high, low], axis=1)

    def second_gram(o):
        lhs = apply_lhs(o)
        for start in range(0, o.nb, 256):
            res = apply_piece(o, lhs, start, 256)
            o.y[:, start : start + 256] = res
            parts = split(res)
            for q in range(3):
                o.sp[q * S : (q + 1) * S, start : start + 256] = parts[q]
        both = dot_nt(o.sp[: 2 * S, :], o.sp[: 2 * S, :])
        cross = dot_nt(o.sp[:S, :], o.sp[2 * S :, :])
        pack(o.i, both[:S, :S] + ((both[:S, S:] + both[S:, :S]) + (both[S:, S:] + (cross + cross.T))))

    def high_dot_nt(lhs, rhs):
        return lax.dot_general(lhs, rhs, NT, precision=lax.Precision.HIGHEST, preferred_element_type=F32)

    def new_left():
        lhs = apply_lhs(left)
        for start in range(0, l_nb, 256):
            res = apply_piece(left, lhs, start, 256)
            l_y[:, start : start + 256] = res
            l_xs[:, start : start + 256] = res.astype(BF16)

    def new_right():
        lhs = apply_lhs(right)
        for h in range(CHUNKS):
            for start in range(h * piece, (h + 1) * piece, 256):
                res = apply_piece(right, lhs, start, 256)
                r_y[:, start : start + 256] = res
                r_xs[h, :, start - h * piece : start - h * piece + 256] = res.astype(BF16)
            later.start(h)

    def multiply(last, after_relay=lambda: None, after_left=lambda: None):
        with jax.named_scope("r_mul0"):
            right_others(last)
        with jax.named_scope("l_relay"):
            left_relay()
            after_relay()
        with jax.named_scope("r_mul1"):
            right_own(last, 0, 2)
        with jax.named_scope("l_fin"):
            left_finish()
        with jax.named_scope("l_mul"):
            left_multiply()
            after_left()
        with jax.named_scope("r_mul2"):
            right_own(last, 2, TILES)

    first, later = Gather(True), Gather(False)
    for h in range(CHUNKS):
        for b in range(piece // S):
            r_xs[h, :, b * S : (b + 1) * S] = r_start[h * piece + b * S : h * piece + (b + 1) * S, :].T.astype(BF16)
        first.start(h)
    for b in range(l_nb // S):
        l_xs[:, b * S : (b + 1) * S] = l_start[b * S : (b + 1) * S, :].T.astype(BF16)
    left_start()
    with jax.named_scope("gather_first"):
        first.finish()
    first.drain()
    l_load.wait()

    def sweep(i, carry):
        multiply(False)
        with jax.named_scope("r_red"):
            right_reduce_finish()
        left_drain()
        pl.when(i > 0)(later.drain)
        with jax.named_scope("factor0"):
            factor(0)
        with jax.named_scope("gram2"):
            hand_over(0, lambda: second_gram(left), lambda: second_gram(right))
        with jax.named_scope("factor1"):
            factor(1)
        with jax.named_scope("new_basis"):
            hand_over(1, new_left, new_right)
            left_start()
        with jax.named_scope("gather"):
            later.finish()
        return carry

    lax.fori_loop(0, SWEEPS, sweep, 0)

    stays = (x == y) & (k == y)

    def swap(c):
        return remote(r_keep.at[0, c], r_keep.at[1, c], es_sem.at[c], er_sem.at[c], 1 - y, col)

    def home(q, c):
        place = 2 * k + (y if q == 0 else 1 - y)
        return remote(r_keep.at[q, c], r_pr.at[c], xs_sem.at[q, c], xr_sem.at[c], y, place)

    direct = (x != y) & (k == y)
    passes_last = (x == y) & (k == y)

    def straight(c):
        return remote(r_keep.at[0, c], r_pr.at[c], xs_sem.at[0, c], xr_sem.at[c], x, 2 * k + y)

    def pass_on(c):
        @pl.when(x == y)
        def _():
            home(1, c).start()

    def own_home(c):
        @pl.when((x == y) & (k != y))
        def _():
            home(0, c).start()

    def after_relay():
        own_home(0)
        own_home(1)

    def after_left():
        swap(0).wait_recv()
        pass_on(0)
        own_home(2)

    for c in range(TILES):
        r_keep[0, c] = r_y[:, c * tile : (c + 1) * tile]
        swap(c).start()
    l_out[...] = l_y[...]
    with jax.named_scope("last_mul"):
        multiply(True, after_relay, after_left)
    with jax.named_scope("ray"):
        total = high_dot_nt(r_keep[1, 0], r_ps[0])
        for c in range(TILES):
            total = total + high_dot_nt(r_keep[0, c], r_y[:, c * tile : (c + 1) * tile])
        for c in range(1, TILES):
            if c == TILES - 1:
                with jax.named_scope("l_red"):
                    left_reduce_finish()
                g_loc[0] = high_dot_nt(l_out[...], l_y[...])
            with jax.named_scope("swap"):
                swap(c).wait_recv()
            if c == 1:
                pass_on(c)
            total = total + high_dot_nt(r_keep[1, c], r_ps[c])
        g_loc[1] = total

    def rest_home():
        own_home(TILES - 1)
        for c in range(STRAIGHT, TILES):

            @pl.when(passes_last)
            def _():
                home(1, c).start()

            @pl.when(direct)
            def _():
                straight(c).start()


    with jax.named_scope("last_sum"):
        g_fac[k] = sum_across(2, S, rest_home)
    left_drain()
    later.drain()
    with jax.named_scope("last_hand"):
        hand_over(2, lambda: None, lambda: None)
    ray_out[...] = g_fac[...]
    with jax.named_scope("home"):
        for c in range(TILES):
            swap(c).wait_send()

            @pl.when(passes_last if c >= STRAIGHT else x == y)
            def _():
                home(1, c).wait_send()

            if c >= STRAIGHT:

                @pl.when(direct)
                def _():
                    straight(c).wait_send()

            @pl.when((x == y) & (k != y))
            def _():
                home(0, c).wait_send()

            @pl.when(stays)
            def _():
                r_out[:, c * tile : (c + 1) * tile] = r_keep[0, c]

            @pl.when(jnp.logical_not(stays))
            def _():
                home(0, c).wait_recv()
                r_out[:, c * tile : (c + 1) * tile] = r_pr[c]


def finish_kernel(l_in, r_in, ray_in, l_out, l_ray, r_out, r_ray):
    for src, dst in ((l_in, l_out), (r_in, r_out)):
        for b in range(dst.shape[0] // S):
            dst[b * S : (b + 1) * S, :] = src[:, b * S : (b + 1) * S].T
    l_ray[...] = ray_in[0]
    r_ray[...] = ray_in[1]


def solution(mesh):
    def local_program(left_op, left_start, right_op, right_start):
        l_nb, r_nb = left_op.shape[0] // 4, right_op.shape[0] // 4
        dma = pltpu.SemaphoreType.DMA
        vmem = pl.BlockSpec(memory_space=pltpu.VMEM)
        hbm = pl.BlockSpec(memory_space=pl.ANY)
        shape = jax.ShapeDtypeStruct
        left_t, right_t, rayleigh = pl.pallas_call(
            kernel,
            out_shape=(shape((S, l_nb), F32), shape((S, r_nb), F32), shape((2, S, S), F32)),
            in_specs=[hbm, vmem, hbm, vmem],
            out_specs=(vmem, vmem, vmem),
            scratch_shapes=[
                pltpu.VMEM(left_op.shape, BF16),
                pltpu.VMEM((RING, right_op.shape[0], r_nb // TILES), BF16),
                pltpu.VMEM((S, l_nb), BF16),
                pltpu.VMEM((2, S, l_nb), BF16),
                pltpu.VMEM((2, S, l_nb), F32),
                pltpu.VMEM((2, S, l_nb), F32),
                pltpu.VMEM((S, l_nb), F32),
                pltpu.VMEM((S, l_nb), F32),
                pltpu.VMEM((S, l_nb), BF16),
                pltpu.VMEM((S, l_nb), F32),
                pltpu.VMEM((3 * S, l_nb), BF16),
                pltpu.VMEM((CHUNKS, S, r_nb // CHUNKS), BF16),
                pltpu.VMEM((4, CHUNKS, S, r_nb // CHUNKS), BF16),
                pltpu.VMEM((TILES, S, r_nb // TILES), F32),
                pltpu.VMEM((TILES, S, r_nb // TILES), F32),
                pltpu.VMEM((S, r_nb), F32),
                pltpu.VMEM((3 * S, r_nb), BF16),
                pltpu.VMEM((2, TILES, S, r_nb // TILES), F32),
                pltpu.VMEM((2, S, S), F32),
                pltpu.VMEM((3, S, S), F32),
                pltpu.VMEM((S, S), F32),
                pltpu.VMEM((3, 3, S, S), F32),
                pltpu.VMEM((S, S), F32),
                pltpu.VMEM((2, S, S), F32),
                dma, dma((RING,)),
                dma((2, CHUNKS)), dma((2, CHUNKS)), dma((2, CHUNKS)), dma((2, CHUNKS)),
                dma((TILES,)), dma((TILES,)), dma((2, TILES)), dma((TILES,)), dma((TILES,)), dma((TILES,)),
                dma((2,)), dma((2,)), dma, dma, dma((2,)), dma((2,)), dma, dma,
                dma((3,)), dma((3,)), dma((3, 3)), dma((3, 3)), dma((3,)), dma((3,)),
            ],
            compiler_params=pltpu.CompilerParams(has_side_effects=True, vmem_limit_bytes=64 * 1024 * 1024 - 65536),
        )(left_op, left_start, right_op, right_start)
        left_basis, left_ray, right_basis, right_ray = pl.pallas_call(
            finish_kernel,
            out_shape=(shape((l_nb, S), F32), shape((S, S), F32), shape((r_nb, S), F32), shape((S, S), F32)),
            in_specs=[vmem] * 3,
            out_specs=(vmem,) * 4,
        )(left_t, right_t, rayleigh)
        return left_basis, left_ray, right_basis, right_ray

    op_spec = P(("batch", "row"), "col")
    vec_spec = P(("batch", "row", "col"), None)
    small_spec = P("batch", None)
    return jax.shard_map(
        local_program, mesh=mesh, in_specs=(op_spec, vec_spec, op_spec, vec_spec),
        out_specs=(vec_spec, small_spec, vec_spec, small_spec), check_vma=False,
    )
```

profile of v0, /device:TPU:0, one launch (start us, length us, event | category | flops | bytes accessed | tf_op | source)
XLA Modules:
  0.0 304.1 jit_solution(17914312238199456726)
XLA Ops:
  0.6 300.7 %shard_map.75 = (f32[128,768]{1,0:T(8,128)}, f32[128,2048]{1,0:T(8,128)}, f32[2,128,128]{2,1,0:T(8,128)}) custom-call(bf16[3072,1536]{1,0:T(8,128)(2,1)} %l_op.1, f32[768,128]{1,0:T(8,128)} %l_start.1, bf16[8192,4096]{1,0:T(8,128)(2,1)} %r_op.1, f32[2048,128]{1,0:T(8,128)} %r_start.1), custom_call_target="tpu_custom_call" | custom-call | tf_op jit(solution)/shard_map/pallas_call | solution.py:606
  301.3 2.8 shard_map.76
where the time goes:
time: 304 us
  Pallas kernels  303 us (100%)
    pallas_call x1, Pallas kernels, local_program(): pl.pallas_call(kernel, out_shape=(shape((S, l_nb), F32), shape((S, r_nb),...  301 us

commit v1 on v0

--- a/solution.py
+++ b/solution.py
@@ -95,7 +95,7 @@
     l_op, l_start, r_op, r_start,
     l_out, r_out, ray_out,
     l_a, r_a,
-    l_xs, l_xt, l_mate_s, l_mate_r, l_side_s, l_side_r, l_hand, l_y, l_sp,
+    l_xs, l_xt, l_mate_s, l_mate_r, l_side_s, l_side_r, l_hand, l_y, l_keep, l_sp,
     r_xs, r_xt, r_ps, r_pr, r_y, r_sp, r_keep,
     g_loc, g_one, g_sum, g_two, g_m, g_fac,
     l_asem, r_asem,
@@ -521,7 +521,7 @@
     for c in range(TILES):
         r_keep[0, c] = r_y[:, c * tile : (c + 1) * tile]
         swap(c).start()
-    l_out[...] = l_y[...]
+    l_keep[...] = l_y[...]
     with jax.named_scope("last_mul"):
         multiply(True, after_relay, after_left)
     with jax.named_scope("ray"):
@@ -532,7 +532,7 @@
             if c == TILES - 1:
                 with jax.named_scope("l_red"):
                     left_reduce_finish()
-                g_loc[0] = high_dot_nt(l_out[...], l_y[...])
+                g_loc[0] = high_dot_nt(l_keep[...], l_y[...])
             with jax.named_scope("swap"):
                 swap(c).wait_recv()
             if c == 1:
@@ -551,6 +551,9 @@
             @pl.when(direct)
             def _():
                 straight(c).start()
+
+        for b in range(0, l_nb, S):
+            l_out[b : b + S, :] = l_keep[:, b : b + S].T
 
 
     with jax.named_scope("last_sum"):
@@ -560,6 +563,11 @@
     with jax.named_scope("last_hand"):
         hand_over(2, lambda: None, lambda: None)
     ray_out[...] = g_fac[...]
+
+    def write(c, src):
+        for b in range(0, tile, S):
+            r_out[c * tile + b : c * tile + b + S, :] = src[:, b : b + S].T
+
     with jax.named_scope("home"):
         for c in range(TILES):
             swap(c).wait_send()
@@ -580,18 +588,17 @@
 
             @pl.when(stays)
             def _():
-                r_out[:, c * tile : (c + 1) * tile] = r_keep[0, c]
+                write(c, r_keep.at[0, c])
 
             @pl.when(jnp.logical_not(stays))
             def _():
                 home(0, c).wait_recv()
-                r_out[:, c * tile : (c + 1) * tile] = r_pr[c]
+                write(c, r_pr.at[c])
 
 
 def finish_kernel(l_in, r_in, ray_in, l_out, l_ray, r_out, r_ray):
-    for src, dst in ((l_in, l_out), (r_in, r_out)):
-        for b in range(dst.shape[0] // S):
-            dst[b * S : (b + 1) * S, :] = src[:, b * S : (b + 1) * S].T
+    l_out[...] = l_in[...]
+    r_out[...] = r_in[...]
     l_ray[...] = ray_in[0]
     r_ray[...] = ray_in[1]
 
@@ -603,9 +610,9 @@
         vmem = pl.BlockSpec(memory_space=pltpu.VMEM)
         hbm = pl.BlockSpec(memory_space=pl.ANY)
         shape = jax.ShapeDtypeStruct
-        left_t, right_t, rayleigh = pl.pallas_call(
+        left_own, right_own, rayleigh = pl.pallas_call(
             kernel,
-            out_shape=(shape((S, l_nb), F32), shape((S, r_nb), F32), shape((2, S, S), F32)),
+            out_shape=(shape((l_nb, S), F32), shape((r_nb, S), F32), shape((2, S, S), F32)),
             in_specs=[hbm, vmem, hbm, vmem],
             out_specs=(vmem, vmem, vmem),
             scratch_shapes=[
@@ -618,6 +625,7 @@
                 pltpu.VMEM((S, l_nb), F32),
                 pltpu.VMEM((S, l_nb), F32),
                 pltpu.VMEM((S, l_nb), BF16),
+                pltpu.VMEM((S, l_nb), F32),
                 pltpu.VMEM((S, l_nb), F32),
                 pltpu.VMEM((3 * S, l_nb), BF16),
                 pltpu.VMEM((CHUNKS, S, r_nb // CHUNKS), BF16),
@@ -646,7 +654,7 @@
             out_shape=(shape((l_nb, S), F32), shape((S, S), F32), shape((r_nb, S), F32), shape((S, S), F32)),
             in_specs=[vmem] * 3,
             out_specs=(vmem,) * 4,
-        )(left_t, right_t, rayleigh)
+        )(left_own, right_own, rayleigh)
         return left_basis, left_ray, right_basis, right_ray
 
     op_spec = P(("batch", "row"), "col")

time: 304 us -> 304 us (level)
  no operation moved by 1% of the time
where the time goes in v1:
time: 304 us
  Pallas kernels  304 us (100%)
    pallas_call x1, Pallas kernels, local_program(): pl.pallas_call(kernel, out_shape=(shape((l_nb, S), F32), shape((r_nb, S),...  301 us

profile of v1, /device:TPU:0, one launch (start us, length us, event | category | flops | bytes accessed | tf_op | source)
XLA Modules:
  0.0 304.3 jit_solution(7258069403899958135)
XLA Ops:
  0.6 301.2 %shard_map.75 = (f32[768,128]{1,0:T(8,128)}, f32[2048,128]{1,0:T(8,128)}, f32[2,128,128]{2,1,0:T(8,128)}) custom-call(bf16[3072,1536]{1,0:T(8,128)(2,1)} %l_op.1, f32[768,128]{1,0:T(8,128)} %l_start.1, bf16[8192,4096]{1,0:T(8,128)(2,1)} %r_op.1, f32[2048,128]{1,0:T(8,128)} %r_start.1), custom_call_target="tpu_custom_call" | custom-call | tf_op jit(solution)/shard_map/pallas_call | solution.py:613
  301.8 2.5 shard_map.76
